TPU v7x, 32 devices: a whole 2x2x4 slice. The times are simulated.
32 devices in a mesh: freq: 4 (over y, x), band: 8 (over z, core).
Axes of the slice: x: 2, y: 2, z: 4, core: 2. Of those that a mesh axis runs over, the one named last changes fastest.
Arguments:
- pair_density: bfloat16 [1024, 2, 8192], P(('freq', 'band')), may hold values from -6 to 6
- trial_vectors: bfloat16 [16, 2, 64, 8192], P('freq', None, None, 'band'), may hold values from -6 to 6
- frequency: float32 [16], P('freq'), may hold values from 0.05 to 20
- val_energy: float32 [32], replicated, may hold values from -3 to -0.1
- cond_energy: float32 [32], replicated, may hold values from 0.1 to 4
- pair_index: int32 [1024], P(('freq', 'band')), may hold values from 0 to 1023, each once
Outputs:
- images: float32 [16, 2, 64, 8192], P('freq', None, None, 'band')
- subspace: float32 [16, 2, 64, 64], P('freq')
Inputs may be any that keep to these rules, and one draw needn't show every extreme that they name: `pair_index`: every pair number 0 to 1023 appears exactly once.
All inputs are finite; a program needn't handle non-finite values.
Results may differ from a plain program's by a relative error of at most 0.0085.
Values may be sent and summed in bfloat16 or wider, within the bound.
No kernel may reach another device: no remote copies, remote signals or barrier semaphores. Data moves between devices by JAX's collectives and lax.ppermute only.
A program may use at most 128 MiB of HBM per device.

v0:
```python
import math
import jax
import jax.numpy as jnp
from jax import lax
from jax.sharding import PartitionSpec as P


def local_weights(pair_index, frequency, val_energy, cond_energy, prefactor):
    cond_count = cond_energy.shape[0]
    val_count = val_energy.shape[0]
    cond_pick = jnp.sum(
        jnp.where(
            (pair_index % cond_count)[:, None] == jnp.arange(cond_count)[None, :],
            cond_energy[None, :],
            0.0,
        ),
        axis=1,
    )
    val_pick = jnp.sum(
        jnp.where(
            (pair_index // cond_count)[:, None] == jnp.arange(val_count)[None, :],
            val_energy[None, :],
            0.0,
        ),
        axis=1,
    )
    delta = cond_pick - val_pick
    ratio = delta[:, None] / (
        delta[:, None] * delta[:, None] + frequency[None, :] * frequency[None, :]
    )
    return (-4.0 * prefactor * ratio).astype(jnp.bfloat16)


def crossing_terms(density, vectors):
    products = jnp.einsum("pcg,fekg->fcekp", density, vectors, preferred_element_type=jnp.float32)
    return jnp.stack(
        [products[:, 0, 0] + products[:, 1, 1], products[:, 0, 1] - products[:, 1, 0]], 1
    )


def scale_terms(crossings, weights):
    factor = jnp.transpose(weights.astype(jnp.float32))[:, None, None, :]
    return (factor * crossings).astype(jnp.bfloat16)


def mix_terms(scaled):
    scaled_real = scaled[:, 0]
    scaled_imag = scaled[:, 1]
    return jnp.stack(
        [jnp.stack([scaled_real, -scaled_imag], 1), jnp.stack([scaled_imag, scaled_real], 1)], 1
    )


def image_terms(density, mixed):
    return jnp.einsum("pcg,fdckp->fdkg", density, mixed, preferred_element_type=jnp.float32)


def shards(pair_density, trial_vectors, frequency, val_energy, cond_energy, pair_index):
    groups = lax.axis_size("freq")
    members = lax.axis_size("band")
    pair_count = pair_density.shape[0] * groups * members
    grid_count = trial_vectors.shape[3] * members
    prefactor = 1.0 / math.sqrt(2.0 * grid_count * pair_count)
    regrouped = lax.all_to_all(pair_density, "band", split_axis=2, concat_axis=0, tiled=True)
    grouped = lax.all_gather(regrouped, "freq", axis=0, tiled=True)
    all_index = lax.all_gather(pair_index, ("freq", "band"), axis=0, tiled=True)
    crossings = crossing_terms(grouped, trial_vectors)
    summed = lax.psum(crossings, "band")
    all_weights = local_weights(all_index, frequency, val_energy, cond_energy, prefactor)
    scaled = scale_terms(summed, all_weights)
    images = image_terms(grouped, mix_terms(scaled))
    vectors = trial_vectors.astype(jnp.float32)
    highest = lax.Precision.HIGHEST
    real_part = jnp.einsum(
        "fkg,flg->fkl", vectors[:, 0], images[:, 0], precision=highest
    ) + jnp.einsum("fkg,flg->fkl", vectors[:, 1], images[:, 1], precision=highest)
    imag_part = jnp.einsum(
        "fkg,flg->fkl", vectors[:, 0], images[:, 1], precision=highest
    ) - jnp.einsum("fkg,flg->fkl", vectors[:, 1], images[:, 0], precision=highest)
    partial_value = jnp.stack([real_part, imag_part], 1) / grid_count
    subspace = lax.psum(partial_value, "band")
    return (images, subspace)


def solution(mesh):
    return jax.shard_map(
        shards,
        mesh=mesh,
        in_specs=(
            P(("freq", "band"), None, None),
            P("freq", None, None, "band"),
            P("freq"),
            P(),
            P(),
            P(("freq", "band")),
        ),
        out_specs=(P("freq", None, None, "band"), P("freq", None, None, None)),
        check_vma=False,
    )
```

profile of v0, /device:TPU:0, one launch (start us, length us, event | category | flops | bytes accessed | tf_op | source)
XLA Modules:
  0.0 269.7 jit_solution(9058504637230988360)
XLA Ops:
  7.2 0.0 all-gather.2.cloned.1.call-start
  7.2 10.8 %copy.31 = bf16[32,2,8192]{0,1,2:T(2,128)(2,1)} copy(bf16[32,2,8192]{2,1,0:T(2,128)(2,1)} %param.6) | data formatting | bytes 2097152 | tf_op args[0]
  18.0 7.0 %reshape.101 = bf16[8,2,32768]{2,1,0:T(2,128)(2,1)S(1)} reshape(bf16[8192,2,32]{2,1,0:T(2,128)(2,1)} %bitcast.76) | data formatting | bytes 2097152
  24.9 32.7 %all_to_all.18 = bf16[8,2,32768]{2,1,0:T(2,128)(2,1)S(1)} all-to-all(bf16[8,2,32768]{2,1,0:T(2,128)(2,1)S(1)} %reshape.101), channel_id=1, replica_groups=mesh['freq'=4,'band'=8] {'band'}, dimensions={0} | all-to-all | bytes 2097152 | tf_op jit(solution)/shard_map/all_to_all | solution.py:64
  57.7 4.5 %reshape.102 = bf16[8192,2,32]{2,1,0:T(2,128)(2,1)} reshape(bf16[8,2,32768]{2,1,0:T(2,128)(2,1)S(1)} %all_to_all.18) | data formatting | bytes 2097152
  62.2 10.5 %copy.32 = bf16[32,2,8,1024]{3,0,2,1:T(8,128)(2,1)} copy(bf16[32,2,8,1024]{0,1,3,2:T(2,128)(2,1)} %bitcast.75) | data formatting | bytes 2097152 | tf_op jit(solution)/shard_map/all_to_all | solution.py:64
  72.6 0.0 all-reduce.4.cloned.1.call-start
  72.7 51.6 %all-gather.2.cloned.1.call-done = bf16[1024,2,1024]{2,0,1:T(8,128)(2,1)} async-done(((bf16[256,2,1024]{2,0,1:T(8,128)(2,1)}), bf16[1024,2,1024]{2,0,1:T(8,128)(2,1)}) %all-gather.2.cloned.1.call-update) | async-done | bytes 4194320 | tf_op jit(solution)/shard_map/all_gather | solution.py:65
  124.3 4.6 %fusion.4 = f32[4,2,2,64,1024]{4,3,1,2,0:T(8,128)S(1)} fusion(bf16[1024,2,1024]{2,0,1:T(8,128)(2,1)} %all-gather.2.cloned.1.call-done, bf16[4,2,64,1024]{3,2,1,0:T(8,128)(2,1)S(1)} %copy-done.1), kind=kOutput, calls=%fused_computation.4 | convolution fusion | flops 2147483648 | bytes 9437184 | tf_op jit(solution)/shard_map/pcg,fekg->fcekp/dot_general | solution.py:35
  128.9 0.1 fusion.15
  129.0 0.1 fusion.17
  129.2 1.5 pad_maximum_fusion
  130.6 0.0 all-reduce.4.cloned.1.call-update
  130.7 0.0 all-reduce.6.cloned.1.call-start
  130.7 0.6 copy-done.5
  131.3 0.2 dynamic-update-slice
  131.5 39.6 %all-reduce = s32[1024]{0:T(1024)S(1)} all-reduce(s32[1024]{0:T(1024)S(1)} %dynamic-update-slice), channel_id=1, replica_groups=mesh['freq'=4,'band'=8] {'freq','band'}, use_global_device_ids=true, to_apply=%add | all-reduce | flops 1024 | bytes 8192
  171.2 0.1 select_reduce_fusion
  171.3 0.1 fusion.29
  171.4 25.1 %all-reduce.4.cloned.1.call-done = f32[4,2,64,1024]{3,2,0,1:T(8,128)} async-done(((f32[4,2,64,1024]{3,2,0,1:T(8,128)}), f32[4,2,64,1024]{3,2,0,1:T(8,128)}) %all-reduce.4.cloned.1.call-update) | async-done | bytes 2097168 | tf_op jit(solution)/shard_map/psum | solution.py:68
  196.5 1.8 multiply_convert_fusion
  198.4 0.1 slice_negate_fusion
  198.5 0.2 maximum_bitcast_fusion
  198.7 1.9 copy-done.4
  200.5 2.3 fusion.8
  202.9 0.6 fusion.20
  203.5 0.6 fusion.19
  204.2 0.6 fusion.13
  204.8 0.6 fusion.14
  205.4 0.7 maximum_multiply_fusion
  206.2 55.2 %all-reduce.6.cloned.1.call-done = f32[4,2,64,64]{2,3,0,1:T(8,128)} async-done(((f32[4,2,64,64]{2,3,0,1:T(8,128)}), f32[4,2,64,64]{2,3,0,1:T(8,128)}) %all-reduce.6.cloned.1.call-update) | async-done | bytes 131088 | tf_op jit(solution)/shard_map/psum | solution.py:81
  261.4 1.8 copy.38
  (18 shorter events, 0.1 us)
Async XLA Ops:
  7.2 117.1 %all-gather.2.cloned.1.call-start = ((), (), s32[]{:S(2)}) async-start(), calls=%async_computation.1 | async-start | bytes 5242880 | tf_op jit(solution)/shard_map/all_gather | solution.py:65
  62.2 62.2 %copy-start.1 = (bf16[4,2,64,1024]{3,2,1,0:T(8,128)(2,1)S(1)}, bf16[4,2,64,1024]{3,2,1,0:T(8,128)(2,1)}, u32[]{:S(2)}) copy-start(bf16[4,2,64,1024]{3,2,1,0:T(8,128)(2,1)} %param.7) | copy-start | bytes 3145732
  72.6 123.9 %all-reduce.4.cloned.1.call-start = ((), (), s32[]{:S(2)}) async-start(), calls=%async_computation.2 | async-start | bytes 4194304 | tf_op jit(solution)/shard_map/psum | solution.py:68
  130.6 0.7 copy-start.5
  130.6 0.7 copy-start.6
  130.6 40.6 %copy-start.2 = (f32[32]{0:T(128)S(1)}, f32[32]{0:T(128)}, u32[]{:S(2)}) copy-start(f32[32]{0:T(128)} %param.9) | copy-start | bytes 388
  130.6 40.6 %copy-start.3 = (f32[32]{0:T(128)S(1)}, f32[32]{0:T(128)}, u32[]{:S(2)}) copy-start(f32[32]{0:T(128)} %param.10) | copy-start | bytes 388
  130.7 130.8 %all-reduce.6.cloned.1.call-start = ((), (), s32[]{:S(2)}) async-start(), calls=%async_computation.3 | async-start | bytes 524288 | tf_op jit(solution)/shard_map/psum | solution.py:81
  198.4 2.2 copy-start.4
  202.9 1.9 copy-start
Sparse Core Ops, SparseCore 0:
  72.8 51.4 all-gather.1
  130.8 65.6 all-reduce.3
  206.3 55.0 all-reduce.5
where the time goes:
time: 271 us; the launch traced here: 270 us
  waiting for transfers between devices  132 us (49%)
  blocking collectives  72.4 us (27%)
  local copies, waits for them, and re-layouts  37.2 us (14%)
  between operations  13.9 us (5%)
  matrix products  9.4 us (3%)
  other arithmetic  4.8 us (2%)
    psum x1, waiting for transfers between devices, shards(): subspace = lax.psum(partial_value, 'band')  55.2 us
    all_gather x1, waiting for transfers between devices, shards(): grouped = lax.all_gather(regrouped, 'freq', axis=0, tiled=True)  51.6 us
    unnamed x1, blocking collectives  39.6 us
    all_to_all x1, blocking collectives, shards(): lax.all_to_all(pair_density, 'band', split_axis=2, concat_axis=0, tiled=T...  32.7 us
    unnamed x20, local copies, waits for them, and re-layouts  26.7 us
    psum x1, waiting for transfers between devices, shards(): summed = lax.psum(crossings, 'band')  25.1 us
    all_to_all x1, local copies, waits for them, and re-layouts, shards(): lax.all_to_all(pair_density, 'band', split_axis=2, concat_axis=0, tiled=T...  10.5 us
  transfers between devices with their start and end apart: 3, of which 3 were waited for; matrix products, arithmetic and copies ran while one was open for 0% of the time, Pallas kernels for 0%

commit v1 on v0

--- a/solution.py
+++ b/solution.py
@@ -61,7 +61,12 @@
     pair_count = pair_density.shape[0] * groups * members
     grid_count = trial_vectors.shape[3] * members
     prefactor = 1.0 / math.sqrt(2.0 * grid_count * pair_count)
-    regrouped = lax.all_to_all(pair_density, "band", split_axis=2, concat_axis=0, tiled=True)
+    regrouped = jnp.concatenate(
+        lax.all_to_all(
+            jnp.stack(jnp.split(pair_density, lax.axis_size("band"), axis=2)), "band", 0, 0
+        ),
+        axis=0,
+    )
     grouped = lax.all_gather(regrouped, "freq", axis=0, tiled=True)
     all_index = lax.all_gather(pair_index, ("freq", "band"), axis=0, tiled=True)
     crossings = crossing_terms(grouped, trial_vectors)

time: 271 us -> 247 us (0.911)
  local copies, waits for them, and re-layouts: 37.2 us -> 13.8 us
    unnamed x20 -> x24, local copies, waits for them, and re-layouts: 26.7 us -> 11.6 us
    all_to_all x1, local copies, waits for them, and re-layouts: 10.5 us -> 1.25 us  [shards(): lax.all_to_all(jnp.stack(jnp.split(pair_density, lax.axis_size('band'), a...]
where the time goes in v1:
time: 247 us
  waiting for transfers between devices  132 us (53%)
  blocking collectives  72.4 us (29%)
  between operations  13.9 us (6%)
  local copies, waits for them, and re-layouts  13.8 us (6%)
  matrix products  9.4 us (4%)
  other arithmetic  4.91 us (2%)
    psum x1, waiting for transfers between devices, shards(): subspace = lax.psum(partial_value, 'band')  55.2 us
    all_gather x1, waiting for transfers between devices, shards(): grouped = lax.all_gather(regrouped, 'freq', axis=0, tiled=True)  51.6 us
    unnamed x1, blocking collectives  39.6 us
    all_to_all x1, blocking collectives, shards(): lax.all_to_all(jnp.stack(jnp.split(pair_density, lax.axis_size('band'), a...  32.7 us
    psum x1, waiting for transfers between devices, shards(): summed = lax.psum(crossings, 'band')  25.1 us
    unnamed x24, local copies, waits for them, and re-layouts  11.6 us
  transfers between devices with their start and end apart: 3, of which 3 were waited for; matrix products, arithmetic and copies ran while one was open for 0% of the time, Pallas kernels for 0%

profile of v1, /device:TPU:0, one launch (start us, length us, event | category | flops | bytes accessed | tf_op | source)
XLA Modules:
  0.0 246.5 jit_solution(2430290449364862297)
XLA Ops:
  7.2 1.0 bitcast_dynamic-update-slice_fusion.7
  8.2 1.0 bitcast_dynamic-update-slice_fusion.6
  9.2 1.0 bitcast_dynamic-update-slice_fusion.5
  10.2 1.0 bitcast_dynamic-update-slice_fusion.4
  11.3 1.0 bitcast_dynamic-update-slice_fusion.3
  12.3 1.0 bitcast_dynamic-update-slice_fusion.2
  13.3 1.0 bitcast_dynamic-update-slice_fusion.1
  14.3 1.0 bitcast_dynamic-update-slice_fusion
  15.3 32.7 %all_to_all.5 = bf16[8,32,2,1024]{3,2,1,0:T(2,128)(2,1)S(1)} all-to-all(bf16[8,32,2,1024]{3,2,1,0:T(2,128)(2,1)S(1)} %bitcast_dynamic-update-slice_fusion), channel_id=1, replica_groups=mesh['freq'=4,'band'=8] {'band'}, dimensions={0} | all-to-all | bytes 2097152 | tf_op jit(solution)/shard_map/all_to_all | solution.py:65
  48.0 1.3 copy.15
  49.4 51.6 %all-gather.2.cloned.1.call-done = bf16[1024,2,1024]{2,0,1:T(8,128)(2,1)} async-done(((bf16[256,2,1024]{2,0,1:T(8,128)(2,1)}), bf16[1024,2,1024]{2,0,1:T(8,128)(2,1)}) %all-gather.2.cloned.1.call-update) | async-done | bytes 4194320 | tf_op jit(solution)/shard_map/all_gather | solution.py:70
  101.0 4.6 %fusion.4 = f32[4,2,2,64,1024]{4,3,2,0,1:T(8,128)S(1)} fusion(bf16[1024,2,1024]{2,0,1:T(8,128)(2,1)} %all-gather.2.cloned.1.call-done, bf16[4,2,64,1024]{3,2,1,0:T(8,128)(2,1)S(1)} %copy-done.1), kind=kOutput, calls=%fused_computation.4 | convolution fusion | flops 2147483648 | bytes 9437184 | tf_op jit(solution)/shard_map/pcg,fekg->fcekp/dot_general | solution.py:35
  105.5 0.1 fusion.15
  105.7 0.2 fusion.17
  105.9 1.5 pad_maximum_fusion
  107.5 0.6 copy-done.5
  108.1 0.2 dynamic-update-slice
  108.3 39.6 %all-reduce = s32[1024]{0:T(1024)S(1)} all-reduce(s32[1024]{0:T(1024)S(1)} %dynamic-update-slice), channel_id=1, replica_groups=mesh['freq'=4,'band'=8] {'freq','band'}, use_global_device_ids=true, to_apply=%add | all-reduce | flops 1024 | bytes 8192
  148.0 0.1 select_reduce_fusion
  148.2 25.1 %all-reduce.4.cloned.1.call-done = f32[4,2,64,1024]{3,2,0,1:T(8,128)} async-done(((f32[4,2,64,1024]{3,2,0,1:T(8,128)}), f32[4,2,64,1024]{3,2,0,1:T(8,128)}) %all-reduce.4.cloned.1.call-update) | async-done | bytes 2097168 | tf_op jit(solution)/shard_map/psum | solution.py:73
  173.3 1.8 multiply_convert_fusion
  175.1 0.1 slice_negate_fusion
  175.3 0.2 maximum_bitcast_fusion
  175.4 1.9 copy-done.4
  177.3 2.3 fusion.8
  179.7 0.6 fusion.20
  180.3 0.6 fusion.19
  180.9 0.6 fusion.13
  181.6 0.6 fusion.14
  182.2 0.7 maximum_multiply_fusion
  183.0 55.2 %all-reduce.6.cloned.1.call-done = f32[4,2,64,64]{2,3,0,1:T(8,128)} async-done(((f32[4,2,64,64]{2,3,0,1:T(8,128)}), f32[4,2,64,64]{2,3,0,1:T(8,128)}) %all-reduce.6.cloned.1.call-update) | async-done | bytes 131088 | tf_op jit(solution)/shard_map/psum | solution.py:86
  238.2 1.8 copy.21
  (23 shorter events, 0.3 us)
Async XLA Ops:
  7.2 93.8 %all-gather.2.cloned.1.call-start = ((), (), s32[]{:S(2)}) async-start(), calls=%async_computation.1 | async-start | bytes 5242880 | tf_op jit(solution)/shard_map/all_gather | solution.py:70
  48.0 52.9 %copy-start.1 = (bf16[4,2,64,1024]{3,2,1,0:T(8,128)(2,1)S(1)}, bf16[4,2,64,1024]{3,2,1,0:T(8,128)(2,1)}, u32[]{:S(2)}) copy-start(bf16[4,2,64,1024]{3,2,1,0:T(8,128)(2,1)} %param.7) | copy-start | bytes 3145732
  49.3 124.0 %all-reduce.4.cloned.1.call-start = ((), (), s32[]{:S(2)}) async-start(), calls=%async_computation.2 | async-start | bytes 4194304 | tf_op jit(solution)/shard_map/psum | solution.py:73
  107.4 0.7 copy-start.5
  107.4 0.7 copy-start.6
  107.4 40.6 %copy-start.2 = (f32[32]{0:T(128)S(1)}, f32[32]{0:T(128)}, u32[]{:S(2)}) copy-start(f32[32]{0:T(128)} %param.9) | copy-start | bytes 388
  107.4 40.6 %copy-start.3 = (f32[32]{0:T(128)S(1)}, f32[32]{0:T(128)}, u32[]{:S(2)}) copy-start(f32[32]{0:T(128)} %param.10) | copy-start | bytes 388
  107.4 130.8 %all-reduce.6.cloned.1.call-start = ((), (), s32[]{:S(2)}) async-start(), calls=%async_computation.3 | async-start | bytes 524288 | tf_op jit(solution)/shard_map/psum | solution.py:86
  175.1 2.2 copy-start.4
  179.7 1.9 copy-start
Sparse Core Ops, SparseCore 0:
  49.4 51.4 all-gather.1
  107.5 65.6 all-reduce.3
  183.1 55.0 all-reduce.5

commit v2 on v0

--- a/solution.py
+++ b/solution.py
@@ -78,7 +78,7 @@
         "fkg,flg->fkl", vectors[:, 0], images[:, 1], precision=highest
     ) - jnp.einsum("fkg,flg->fkl", vectors[:, 1], images[:, 0], precision=highest)
     partial_value = jnp.stack([real_part, imag_part], 1) / grid_count
-    subspace = lax.psum(partial_value, "band")
+    subspace = jnp.sum(lax.all_gather(partial_value, "band"), axis=0)
     return (images, subspace)
 
 

time: 271 us -> 246 us (0.908)
  waiting for transfers between devices: 132 us -> 106 us
    psum x1 -> x0, waiting for transfers between devices: 55.2 us -> none  [shards(): subspace = lax.psum(partial_value, 'band')]
    all_gather x0 -> x1, waiting for transfers between devices: none -> 28.9 us  [shards(): subspace = jnp.sum(lax.all_gather(partial_value, 'band'), axis=0)]
    unnamed x20 -> x19, local copies, waits for them, and re-layouts: 26.7 us -> 24.9 us
where the time goes in v2:
time: 246 us; the launch traced here: 244 us
  waiting for transfers between devices  106 us (43%)
  blocking collectives  72.3 us (29%)
  local copies, waits for them, and re-layouts  36.2 us (15%)
  between operations  13.9 us (6%)
  matrix products  9.4 us (4%)
  other arithmetic  6.63 us (3%)
    all_gather x1, waiting for transfers between devices, shards(): grouped = lax.all_gather(regrouped, 'freq', axis=0, tiled=True)  51.6 us
    unnamed x1, blocking collectives  39.6 us
    all_to_all x1, blocking collectives, shards(): lax.all_to_all(pair_density, 'band', split_axis=2, concat_axis=0, tiled=T...  32.7 us
    all_gather x1, waiting for transfers between devices, shards(): subspace = jnp.sum(lax.all_gather(partial_value, 'band'), axis=0)  28.9 us
    psum x1, waiting for transfers between devices, shards(): summed = lax.psum(crossings, 'band')  25.2 us
    unnamed x19, local copies, waits for them, and re-layouts  24.9 us
    all_to_all x1, local copies, waits for them, and re-layouts, shards(): lax.all_to_all(pair_density, 'band', split_axis=2, concat_axis=0, tiled=T...  10.5 us
  transfers between devices with their start and end apart: 3, of which 3 were waited for; matrix products, arithmetic and copies ran while one was open for 0% of the time, Pallas kernels for 0%

profile of v2, /device:TPU:0, one launch (start us, length us, event | category | flops | bytes accessed | tf_op | source)
XLA Modules:
  0.0 244.3 jit_solution(1319014893914900127)
XLA Ops:
  7.2 0.0 all-gather.3.cloned.1.call-start
  7.2 10.8 %copy.34 = bf16[32,2,8192]{0,1,2:T(2,128)(2,1)} copy(bf16[32,2,8192]{2,1,0:T(2,128)(2,1)} %param.6) | data formatting | bytes 2097152 | tf_op args[0]
  18.0 7.0 %reshape.132 = bf16[8,2,32768]{2,1,0:T(2,128)(2,1)S(1)} reshape(bf16[8192,2,32]{2,1,0:T(2,128)(2,1)} %bitcast.76) | data formatting | bytes 2097152
  25.0 32.7 %all_to_all.18 = bf16[8,2,32768]{2,1,0:T(2,128)(2,1)S(1)} all-to-all(bf16[8,2,32768]{2,1,0:T(2,128)(2,1)S(1)} %reshape.132), channel_id=1, replica_groups=mesh['freq'=4,'band'=8] {'band'}, dimensions={0} | all-to-all | bytes 2097152 | tf_op jit(solution)/shard_map/all_to_all | solution.py:64
  57.7 4.5 %reshape.133 = bf16[8192,2,32]{2,1,0:T(2,128)(2,1)} reshape(bf16[8,2,32768]{2,1,0:T(2,128)(2,1)S(1)} %all_to_all.18) | data formatting | bytes 2097152
  62.2 10.5 %copy.35 = bf16[32,2,8,1024]{3,0,2,1:T(8,128)(2,1)} copy(bf16[32,2,8,1024]{0,1,3,2:T(2,128)(2,1)} %bitcast.75) | data formatting | bytes 2097152 | tf_op jit(solution)/shard_map/all_to_all | solution.py:64
  72.6 0.0 all-reduce.3.cloned.1.call-start
  72.7 51.6 %all-gather.3.cloned.1.call-done = bf16[1024,2,1024]{2,0,1:T(8,128)(2,1)} async-done(((bf16[256,2,1024]{2,0,1:T(8,128)(2,1)}), bf16[1024,2,1024]{2,0,1:T(8,128)(2,1)}) %all-gather.3.cloned.1.call-update) | async-done | bytes 4194320 | tf_op jit(solution)/shard_map/all_gather | solution.py:65
  124.3 4.6 %fusion.4 = f32[4,2,2,64,1024]{4,3,1,2,0:T(8,128)S(1)} fusion(bf16[1024,2,1024]{2,0,1:T(8,128)(2,1)} %all-gather.3.cloned.1.call-done, bf16[4,2,64,1024]{3,2,1,0:T(8,128)(2,1)S(1)} %copy-done.1), kind=kOutput, calls=%fused_computation.4 | convolution fusion | flops 2147483648 | bytes 9437184 | tf_op jit(solution)/shard_map/pcg,fekg->fcekp/dot_general | solution.py:35
  128.9 0.1 fusion.15
  129.0 0.1 fusion.17
  129.2 1.5 pad_maximum_fusion
  130.6 0.0 all-reduce.3.cloned.1.call-update
  130.7 0.0 all-gather.5.cloned.1.call-start
  130.7 0.6 copy-done.5
  131.3 0.2 dynamic-update-slice
  131.5 39.6 %all-reduce = s32[1024]{0:T(1024)S(1)} all-reduce(s32[1024]{0:T(1024)S(1)} %dynamic-update-slice), channel_id=1, replica_groups=mesh['freq'=4,'band'=8] {'freq','band'}, use_global_device_ids=true, to_apply=%add | all-reduce | flops 1024 | bytes 8192
  171.1 0.1 select_reduce_fusion
  171.3 0.1 fusion.29
  171.4 25.2 %all-reduce.3.cloned.1.call-done = f32[4,2,64,1024]{3,2,0,1:T(8,128)} async-done(((f32[4,2,64,1024]{3,2,0,1:T(8,128)}), f32[4,2,64,1024]{3,2,0,1:T(8,128)}) %all-reduce.3.cloned.1.call-update) | async-done | bytes 2097168 | tf_op jit(solution)/shard_map/psum | solution.py:68
  196.5 1.8 multiply_convert_fusion
  198.4 0.1 slice_negate_fusion
  198.5 0.2 maximum_bitcast_fusion
  198.7 1.9 copy-done.4
  200.6 2.3 fusion.8
  202.9 0.6 fusion.20
  203.6 0.6 fusion.19
  204.2 0.6 fusion.13
  204.8 0.6 fusion.14
  205.5 0.8 copy.41
  206.4 28.9 %all-gather.5.cloned.1.call-done = f32[8,4,2,64,64]{4,3,2,1,0:T(8,128)} async-done(((f32[1,4,2,64,64]{4,3,2,1,0:T(8,128)}), f32[8,4,2,64,64]{4,3,2,1,0:T(8,128)}) %all-gather.5.cloned.1.call-update) | async-done | bytes 1048592 | tf_op jit(solution)/shard_map/all_gather | solution.py:81
  235.3 2.5 %reduce_sum.29 = f32[4,2,64,64]{3,2,1,0:T(8,128)} reduce(f32[8,4,2,64,64]{4,3,2,1,0:T(8,128)} %all-gather.5.cloned.1.call-done, f32[]{:T(128)} %constant.29.clone.1), dimensions={0}, to_apply=%region_3.4 | reduce | flops 229376 | bytes 1179652 | tf_op jit(solution)/shard_map/reduce_sum | solution.py:81
  (19 shorter events, 0.1 us)
Async XLA Ops:
  7.2 117.1 %all-gather.3.cloned.1.call-start = ((), (), s32[]{:S(2)}) async-start(), calls=%async_computation.1 | async-start | bytes 5242880 | tf_op jit(solution)/shard_map/all_gather | solution.py:65
  62.2 62.2 %copy-start.1 = (bf16[4,2,64,1024]{3,2,1,0:T(8,128)(2,1)S(1)}, bf16[4,2,64,1024]{3,2,1,0:T(8,128)(2,1)}, u32[]{:S(2)}) copy-start(bf16[4,2,64,1024]{3,2,1,0:T(8,128)(2,1)} %param.7) | copy-start | bytes 3145732
  72.6 123.9 %all-reduce.3.cloned.1.call-start = ((), (), s32[]{:S(2)}) async-start(), calls=%async_computation.2 | async-start | bytes 4194304 | tf_op jit(solution)/shard_map/psum | solution.py:68
  130.6 0.7 copy-start.5
  130.6 0.7 copy-start.6
  130.6 40.5 %copy-start.2 = (f32[32]{0:T(128)S(1)}, f32[32]{0:T(128)}, u32[]{:S(2)}) copy-start(f32[32]{0:T(128)} %param.9) | copy-start | bytes 388
  130.6 40.5 %copy-start.3 = (f32[32]{0:T(128)S(1)}, f32[32]{0:T(128)}, u32[]{:S(2)}) copy-start(f32[32]{0:T(128)} %param.10) | copy-start | bytes 388
  130.7 104.6 %all-gather.5.cloned.1.call-start = ((), (), s32[]{:S(2)}) async-start(), calls=%async_computation.3 | async-start | bytes 2359296 | tf_op jit(solution)/shard_map/all_gather | solution.py:81
  198.4 2.2 copy-start.4
  202.9 1.9 copy-start
Sparse Core Ops, SparseCore 0:
  72.8 51.4 all-gather.2
  130.8 65.7 all-reduce.2
  206.5 28.7 all-gather.4
